TPU v7x, 16 devices: a whole 2x2x2 slice. The times are simulated.
16 devices in a mesh: data: 16 (over z, y, x, core).
Axes of the slice: x: 2, y: 2, z: 2, core: 2. Of those that a mesh axis runs over, the one named last changes fastest.
Arguments:
- x_in: bfloat16 [384, 64, 1280], P('data')
- g_out: bfloat16 [384, 64, 1280], P('data')
- step_emb: bfloat16 [2, 1280], replicated
- w_q: bfloat16 [1280, 20, 64], replicated
- w_k: bfloat16 [1280, 20, 64], replicated
- w_v: bfloat16 [1280, 20, 64], replicated
- w_o: bfloat16 [20, 64, 1280], replicated
- w_up: bfloat16 [1280, 5120], replicated
- w_down: bfloat16 [5120, 1280], replicated
Outputs:
- output 1: float32 [1280, 20, 64], replicated
- output 2: float32 [1280, 20, 64], replicated
- output 3: float32 [1280, 20, 64], replicated
- output 4: float32 [20, 64, 1280], replicated
- output 5: float32 [1280, 5120], replicated
- output 6: float32 [5120, 1280], replicated
- output 7: bfloat16 [384, 64, 1280], P('data')
All inputs are finite; a program needn't handle non-finite values.
Results may differ from a plain program's by a relative error of at most 0.02.
Values are sent between devices in bfloat16 or wider.
A program may use at most 1 GiB of HBM per device.

v0:
```python
import jax
import jax.numpy as jnp
from jax import lax
from jax.sharding import PartitionSpec as P, NamedSharding
import functools

NORM_EPS = 1e-6


def rms_norm(x_val):
    x_f32 = x_val.astype(jnp.float32)
    return (x_f32 * lax.rsqrt(jnp.mean(x_f32 * x_f32, axis=-1, keepdims=True) + NORM_EPS)).astype(jnp.bfloat16)


def gelu_act(z_val):
    return jax.nn.gelu(z_val.astype(jnp.float32), approximate=True).astype(jnp.bfloat16)


def attn_probs(scores, attn_scale):
    return jax.nn.softmax(scores.astype(jnp.float32) * attn_scale, axis=-1).astype(jnp.bfloat16)


def layer_fwd(x_prev, step_vec, weight_set, attn_scale):
    w_qkv, w_o, w_up, w_down = weight_set
    n_heads = w_o.shape[0]
    x_cur = x_prev + step_vec
    u_norm = rms_norm(x_cur)
    qkv_heads = jnp.einsum('bsd,dhe->bshe', u_norm, w_qkv, preferred_element_type=jnp.float32).astype(jnp.bfloat16)
    q_heads = qkv_heads[:, :, :n_heads]
    k_heads = qkv_heads[:, :, n_heads:2 * n_heads]
    v_heads = qkv_heads[:, :, 2 * n_heads:]
    scores = jnp.einsum('bqhe,bkhe->bhqk', q_heads, k_heads, preferred_element_type=jnp.float32).astype(jnp.bfloat16)
    prob_mat = attn_probs(scores, attn_scale)
    mix_heads = jnp.einsum('bhqk,bkhe->bqhe', prob_mat, v_heads, preferred_element_type=jnp.float32).astype(jnp.bfloat16)
    attn_out = jnp.einsum('crif,ife->cre', mix_heads, w_o, preferred_element_type=jnp.float32).astype(jnp.bfloat16)
    h_mid = x_cur + attn_out
    z_up = jnp.dot(rms_norm(h_mid), w_up, preferred_element_type=jnp.float32).astype(jnp.bfloat16)
    y_down = jnp.dot(gelu_act(z_up), w_down, preferred_element_type=jnp.float32).astype(jnp.bfloat16)
    return h_mid + y_down, (x_cur, qkv_heads, mix_heads, h_mid, z_up)


def layer_bwd(d_out, saved_acts, weight_set, attn_scale):
    w_qkv, w_o, w_up, w_down = weight_set
    x_cur, qkv_heads, mix_heads, h_mid, z_up = saved_acts
    n_heads = w_o.shape[0]
    g_act, gelu_pull = jax.vjp(gelu_act, z_up)
    grad_down = jnp.einsum('bsf,bsd->fd', g_act, d_out, preferred_element_type=jnp.float32)
    d_act = jnp.einsum('bsd,fd->bsf', d_out, w_down, preferred_element_type=jnp.float32).astype(jnp.bfloat16)
    (d_up,) = gelu_pull(d_act)
    m_norm, norm_pull_h = jax.vjp(rms_norm, h_mid)
    grad_up = jnp.einsum('bsd,bsf->df', m_norm, d_up, preferred_element_type=jnp.float32)
    d_norm_h = jnp.einsum('bsf,df->bsd', d_up, w_up, preferred_element_type=jnp.float32).astype(jnp.bfloat16)
    (d_mid_norm,) = norm_pull_h(d_norm_h)
    d_mid = d_out + d_mid_norm
    grad_o = jnp.einsum('crif,cre->ife', mix_heads, d_mid, preferred_element_type=jnp.float32)
    d_mix = jnp.einsum('cre,ife->crif', d_mid, w_o, preferred_element_type=jnp.float32).astype(jnp.bfloat16)
    q_heads = qkv_heads[:, :, :n_heads]
    k_heads = qkv_heads[:, :, n_heads:2 * n_heads]
    v_heads = qkv_heads[:, :, 2 * n_heads:]
    scores = jnp.einsum('bqhe,bkhe->bhqk', q_heads, k_heads, preferred_element_type=jnp.float32).astype(jnp.bfloat16)
    prob_mat, prob_pull = jax.vjp(functools.partial(attn_probs, attn_scale=attn_scale), scores)
    d_v = jnp.einsum('bhqk,bqhe->bkhe', prob_mat, d_mix, preferred_element_type=jnp.float32).astype(jnp.bfloat16)
    d_prob = jnp.einsum('bqhe,bkhe->bhqk', d_mix, v_heads, preferred_element_type=jnp.float32).astype(jnp.bfloat16)
    (d_scores,) = prob_pull(d_prob)
    d_q = jnp.einsum('bhqk,bkhe->bqhe', d_scores, k_heads, preferred_element_type=jnp.float32).astype(jnp.bfloat16)
    d_k = jnp.einsum('bhqk,bqhe->bkhe', d_scores, q_heads, preferred_element_type=jnp.float32).astype(jnp.bfloat16)
    d_qkv = jnp.concatenate([d_q, d_k, d_v], axis=2)
    u_norm, norm_pull_x = jax.vjp(rms_norm, x_cur)
    grad_qkv = jnp.einsum('bsd,bshe->dhe', u_norm, d_qkv, preferred_element_type=jnp.float32)
    d_norm_x = jnp.einsum('bshe,dhe->bsd', d_qkv, w_qkv, preferred_element_type=jnp.float32).astype(jnp.bfloat16)
    (d_cur_norm,) = norm_pull_x(d_norm_x)
    return d_mid + d_cur_norm, (grad_qkv, grad_o, grad_up, grad_down)


def micro_pass(x_mb, g_mb, step_emb, weight_set, attn_scale):
    n_layers = step_emb.shape[0]
    x_cur = x_mb
    saved_list = []
    for layer_idx in range(n_layers):
        x_cur, saved_acts = layer_fwd(x_cur, step_emb[layer_idx], weight_set, attn_scale)
        saved_list.append(saved_acts)
    d_cur = g_mb
    grad_sum = tuple(jnp.zeros(w.shape, jnp.float32) for w in weight_set)
    for layer_idx in reversed(range(n_layers)):
        d_cur, layer_grads = layer_bwd(d_cur, saved_list[layer_idx], weight_set, attn_scale)
        grad_sum = tuple(acc_part + new_part for acc_part, new_part in zip(grad_sum, layer_grads))
    return d_cur, grad_sum


def solution(mesh):
    batch_spec = P('data', None, None)

    def per_device(x_loc, g_loc, step_emb, w_q, w_k, w_v, w_o, w_up, w_down):
        n_heads = w_q.shape[1]
        attn_scale = w_q.shape[2] ** -0.5
        weight_set = (jnp.concatenate([w_q, w_k, w_v], axis=1), w_o, w_up, w_down)
        rows_mb = x_loc.shape[0] // 2
        dx_parts = []
        grad_total = tuple(jnp.zeros(w.shape, jnp.float32) for w in weight_set)
        for micro_idx in range(2):
            start_row = micro_idx * rows_mb
            d_x, micro_grads = micro_pass(x_loc[start_row:start_row + rows_mb], g_loc[start_row:start_row + rows_mb], step_emb, weight_set, attn_scale)
            reduced = lax.psum(micro_grads, 'data')
            grad_total = tuple(acc_part + new_part for acc_part, new_part in zip(grad_total, reduced))
            dx_parts.append(d_x)
        grad_qkv, grad_o, grad_up, grad_down = grad_total
        return (grad_qkv[:, :n_heads], grad_qkv[:, n_heads:2 * n_heads], grad_qkv[:, 2 * n_heads:], grad_o, grad_up, grad_down, jnp.concatenate(dx_parts, axis=0))

    return jax.shard_map(per_device, mesh=mesh, in_specs=(batch_spec, batch_spec, P(), P(), P(), P(), P(), P(), P()), out_specs=(P(), P(), P(), P(), P(), P(), batch_spec), check_vma=False)
```

profile of v0, /device:TPU:0, one launch (start us, length us, event | category | flops | bytes accessed | tf_op | source)
XLA Modules:
  0.0 1798.5 jit_solution(17918929040555146088)
XLA Ops:
  7.2 17.7 fusion.97
  24.9 17.5 fusion.91
  46.4 19.2 %convolution_convert_fusion.1 = bf16[12,64,60,64]{3,1,2,0:T(8,128)(2,1)S(1)} fusion(f32[12,64]{1,0:T(8,128)S(1)} %fusion.369, bf16[24,64,1280]{2,1,0:T(8,128)(2,1)} %param.9, bf16[1280]{0:T(1024)(128)(2,1)S(1)} %get-tuple-element.12, bf16[1280,20,64]{0,2,1:T(8,128)(2,1)} %param.14, bf16[1280,20,64]{0,2,1:T(8,128)(2,1)} %param.13, ...), kind=kOutput, calls=%fused_computation.213 | convolution fusion | flops 7588085760 | bytes 17700352 | tf_op jit(solution)/shard_map/bsd,dhe->bshe/dot_general | solution.py:28
  81.0 7.7 convolution_convert_fusion.5
  96.5 16.1 fusion.85
  112.7 21.4 %fusion.177 = (f32[12,64]{1,0:T(8,128)S(1)}, bf16[12,64,1280]{2,1,0:T(8,128)(2,1)S(1)}) fusion(bf16[1280]{0:T(1024)(128)(2,1)S(1)} %get-tuple-element.11, bf16[12,64,1280]{2,1,0:T(8,128)(2,1)S(1)} %copy-done.18, bf16[5120,1280]{1,0:T(8,128)(2,1)} %param.17, bf16[12,64,5120]{2,1,0:T(8,128)(2,1)S(1)} %fusion.85), kind=kOutput, calls=%fused_computation.268 | convolution fusion | flops 10111548416 | bytes 24909312 | tf_op jit(solution)/shard_map/dot_general | solution.py:38
  135.4 19.7 %convolution_convert_fusion = bf16[12,64,60,64]{3,1,2,0:T(8,128)(2,1)S(1)} fusion(bf16[12,64,1280]{2,1,0:T(8,128)(2,1)S(1)} %get-tuple-element.41, f32[12,64]{1,0:T(8,128)S(1)} %fusion.371, bf16[1280,20,64]{0,2,1:T(8,128)(2,1)S(1)} %copy-done.91, bf16[1280,20,64]{0,2,1:T(8,128)(2,1)} %param.13, bf16[1280,20,64]{0,2,1:T(8,128)(2,1)} %param.12), kind=kOutput, calls=%fused_computation.212 | convolution fusion | flops 7585136640 | bytes 17697792 | tf_op jit(solution)/shard_map/bsd,dhe->bshe/dot_general | solution.py:28
  170.4 7.7 convolution_convert_fusion.4
  185.3 17.4 fusion.88
  202.6 30.0 %fusion.182 = (f32[12,64]{1,0:T(8,128)S(1)}, bf16[12,64,1280]{2,1,0:T(8,128)(2,1)}) fusion(bf16[12,64,1280]{2,1,0:T(8,128)(2,1)} %copy-done.22, bf16[1280,5120]{1,0:T(8,128)(2,1)} %param.16, bf16[12,64,5120]{2,1,0:T(8,128)(2,1)} %fusion.97, bf16[12,64,5120]{2,1,0:T(8,128)(2,1)} %fusion.88), kind=kOutput, calls=%fused_computation.273 | convolution fusion | flops 10157751296 | bytes 32771072 | tf_op jit(solution)/shard_map/bsf,df->bsd/dot_general | solution.py:52
  233.2 19.2 %convolution_convert_fusion.3 = bf16[12,64,60,64]{3,1,2,0:T(8,128)(2,1)S(1)} fusion(f32[12,64]{1,0:T(8,128)S(1)} %copy-done.60, bf16[24,64,1280]{2,1,0:T(8,128)(2,1)} %param.9, bf16[1280]{0:T(1024)(128)(2,1)S(1)} %copy-done.57, bf16[1280,20,64]{0,2,1:T(8,128)(2,1)} %param.14, bf16[1280,20,64]{0,2,1:T(8,128)(2,1)} %param.13, bf16[1280,20,64]{0,2,1:T(8,128)(2,1)} %param.12), kind=kOutput, calls=%fused_computation.215 | convolution fusion | flops 7588085760 | bytes 17700352 | tf_op jit(solution)/shard_map/bsd,dhe->bshe/dot_general | solution.py:28
  268.0 7.7 convolution_convert_fusion.7
  281.8 14.2 fusion.79
  296.0 21.4 %fusion.165 = (f32[12,64]{1,0:T(8,128)S(1)}, bf16[12,64,1280]{2,1,0:T(8,128)(2,1)S(1)}) fusion(bf16[1280]{0:T(1024)(128)(2,1)S(1)} %copy-done.90, bf16[12,64,1280]{2,1,0:T(8,128)(2,1)S(1)} %get-tuple-element.27, bf16[5120,1280]{1,0:T(8,128)(2,1)} %param.17, bf16[12,64,5120]{2,1,0:T(8,128)(2,1)S(1)} %fusion.79), kind=kOutput, calls=%fused_computation.256 | convolution fusion | flops 10111548416 | bytes 24909312 | tf_op jit(solution)/shard_map/dot_general | solution.py:38
  318.7 19.6 %convolution_convert_fusion.2 = bf16[12,64,60,64]{3,1,2,0:T(8,128)(2,1)S(1)} fusion(bf16[12,64,1280]{2,1,0:T(8,128)(2,1)S(1)} %get-tuple-element.29, f32[12,64]{1,0:T(8,128)S(1)} %fusion.367, bf16[1280,20,64]{0,2,1:T(8,128)(2,1)S(1)} %copy-done.92, bf16[1280,20,64]{0,2,1:T(8,128)(2,1)} %param.13, bf16[1280,20,64]{0,2,1:T(8,128)(2,1)} %param.12), kind=kOutput, calls=%fused_computation.214 | convolution fusion | flops 7585136640 | bytes 17697792 | tf_op jit(solution)/shard_map/bsd,dhe->bshe/dot_general | solution.py:28
  353.3 8.5 convolution_convert_fusion.6
  368.9 17.4 fusion.82
  386.3 30.0 %fusion.170 = (f32[12,64]{1,0:T(8,128)S(1)}, bf16[12,64,1280]{2,1,0:T(8,128)(2,1)}) fusion(bf16[12,64,1280]{2,1,0:T(8,128)(2,1)} %copy-done.24, bf16[1280,5120]{1,0:T(8,128)(2,1)} %param.16, bf16[12,64,5120]{2,1,0:T(8,128)(2,1)} %fusion.91, bf16[12,64,5120]{2,1,0:T(8,128)(2,1)} %fusion.82), kind=kOutput, calls=%fused_computation.261 | convolution fusion | flops 10157751296 | bytes 32771072 | tf_op jit(solution)/shard_map/bsf,df->bsd/dot_general | solution.py:52
  441.0 9.7 fusion.111
  471.4 8.1 fusion.199
  492.5 9.7 fusion.121
  520.1 14.3 fusion.179
  534.4 14.4 fusion.146
  548.8 14.4 fusion.167
  563.3 14.6 fusion.150
  580.4 17.5 fusion.100
  598.0 30.4 %fusion.176 = (f32[12,64]{1,0:T(8,128)S(1)}, bf16[12,64,1280]{2,1,0:T(8,128)(2,1)}) fusion(bf16[12,64,1280]{2,1,0:T(8,128)(2,1)} %get-tuple-element.39, bf16[1280,5120]{1,0:T(8,128)(2,1)} %param.16, bf16[12,64,5120]{2,1,0:T(8,128)(2,1)} %fusion.100, bf16[12,64,5120]{2,1,0:T(8,128)(2,1)} %copy-done.7), kind=kOutput, calls=%fused_computation.267 | convolution fusion | flops 10157751296 | bytes 32771072 | tf_op jit(solution)/shard_map/bsf,df->bsd/dot_general | solution.py:52
  646.8 9.7 fusion.126
  676.5 17.7 fusion.94
  694.2 30.0 %fusion.164 = (f32[12,64]{1,0:T(8,128)S(1)}, bf16[12,64,1280]{2,1,0:T(8,128)(2,1)}) fusion(bf16[12,64,1280]{2,1,0:T(8,128)(2,1)} %copy-done.25, bf16[1280,5120]{1,0:T(8,128)(2,1)} %param.16, bf16[12,64,5120]{2,1,0:T(8,128)(2,1)} %fusion.94, bf16[12,64,5120]{2,1,0:T(8,128)(2,1)} %copy-done.103), kind=kOutput, calls=%fused_computation.255 | convolution fusion | flops 10157751296 | bytes 32771072 | tf_op jit(solution)/shard_map/bsf,df->bsd/dot_general | solution.py:52
  746.5 9.7 fusion.116
  773.6 27.2 %fusion.354 = f32[1280,5120,1]{1,0,2:T(8,128)} fusion(bf16[12,64,1280]{2,1,0:T(8,128)(2,1)} %copy-done.25, f32[12,64]{1,0:T(8,128)S(1)} %copy-done.79, bf16[12,64,5120]{2,1,0:T(8,128)(2,1)} %fusion.94, bf16[12,64,5120]{2,1,0:T(8,128)(2,1)} %copy-done.103), kind=kOutput, calls=%fused_computation.398 | convolution fusion | flops 10155786240 | bytes 43912192 | tf_op jit(solution)/shard_map/bsd,bsf->df/dot_general | solution.py:51
  800.8 26.6 %fusion.346 = f32[1280,5120,1]{1,0,2:T(8,128)} fusion(bf16[12,64,1280]{2,1,0:T(8,128)(2,1)S(1)} %copy-done.23, f32[12,64]{1,0:T(8,128)S(1)} %copy-done.67, bf16[12,64,5120]{2,1,0:T(8,128)(2,1)} %fusion.97, bf16[12,64,5120]{2,1,0:T(8,128)(2,1)} %fusion.88), kind=kOutput, calls=%fused_computation.396 | convolution fusion | flops 10155786240 | bytes 43912192 | tf_op jit(solution)/shard_map/bsd,bsf->df/dot_general | solution.py:51
  827.5 27.0 %fusion.351 = f32[1280,5120,1]{1,0,2:T(8,128)} fusion(bf16[12,64,1280]{2,1,0:T(8,128)(2,1)} %copy-done.24, f32[12,64]{1,0:T(8,128)S(1)} %copy-done.69, bf16[12,64,5120]{2,1,0:T(8,128)(2,1)} %fusion.91, bf16[12,64,5120]{2,1,0:T(8,128)(2,1)} %fusion.82), kind=kOutput, calls=%fused_computation.397 | convolution fusion | flops 10155786240 | bytes 43912192 | tf_op jit(solution)/shard_map/bsd,bsf->df/dot_general | solution.py:51
  854.4 20.8 %fusion.395 = f32[5120,1280,1]{1,0,2:T(8,128)} fusion(bf16[12,64,1280]{2,1,0:T(8,128)(2,1)S(1)} %copy-done.17, bf16[12,64,5120]{2,1,0:T(8,128)(2,1)} %copy-done.103), kind=kOutput, calls=%fused_computation.449 | convolution fusion | flops 10105651200 | bytes 36044800 | tf_op jit(solution)/shard_map/bsf,bsd->fd/dot_general | solution.py:47
  875.2 20.1 %fusion.105 = f32[5120,1280,1]{1,0,2:T(8,128)} fusion(bf16[12,64,5120]{2,1,0:T(8,128)(2,1)} %fusion.82, bf16[24,64,1280]{2,1,0:T(8,128)(2,1)S(1)} %copy-done.20), kind=kOutput, calls=%fused_computation.131 | convolution fusion | flops 10105651200 | bytes 36044800 | tf_op jit(solution)/shard_map/bsf,bsd->fd/dot_general | solution.py:47
  895.3 20.3 %fusion.103 = f32[5120,1280,1]{1,0,2:T(8,128)} fusion(bf16[12,64,5120]{2,1,0:T(8,128)(2,1)} %fusion.88, bf16[24,64,1280]{2,1,0:T(8,128)(2,1)S(1)} %copy-done.20), kind=kOutput, calls=%fused_computation.130 | convolution fusion | flops 10105651200 | bytes 36044800 | tf_op jit(solution)/shard_map/bsf,bsd->fd/dot_general | solution.py:47
  915.7 10.7 fusion.143
  928.1 13.4 fusion.148
  941.5 45.5 %fusion.5 = f32[1280,5120]{1,0:T(8,128)} fusion(f32[1280,5120,1]{1,0,2:T(8,128)} %fusion.346, f32[1280,5120,1]{1,0,2:T(8,128)} %fusion.354, f32[1280,5120,1]{1,0,2:T(8,128)} %fusion.351, bf16[12,64,1280]{2,1,0:T(8,128)(2,1)} %get-tuple-element.39, f32[12,64]{1,0:T(8,128)S(1)} %copy-done.40, bf16[12,64,5120]{2,1,0:T(8,128)(2,1)} %fusion.100, ...), kind=kOutput, calls=%fused_computation.28 | convolution fusion | flops 10175447040 | bytes 122555392 | tf_op jit(solution)/shard_map/bsd,bsf->df/dot_general | solution.py:51
  987.0 40.2 %fusion.4 = f32[5120,1280]{1,0:T(8,128)} fusion(f32[5120,1280,1]{1,0,2:T(8,128)} %fusion.103, f32[5120,1280,1]{1,0,2:T(8,128)} %fusion.395, f32[5120,1280,1]{1,0,2:T(8,128)} %fusion.105, bf16[12,64,1280]{2,1,0:T(8,128)(2,1)} %fusion.331, bf16[12,64,5120]{2,1,0:T(8,128)(2,1)} %copy-done.7), kind=kOutput, calls=%fused_computation.25 | convolution fusion | flops 10125312000 | bytes 114688000 | tf_op jit(solution)/shard_map/bsf,bsd->fd/dot_general | solution.py:47
  1027.3 32.5 %fusion.10 = f32[1280,60,64]{0,2,1:T(8,128)} fusion(f32[1280,60,64,1]{0,2,1,3:T(8,128)} %fusion.146, f32[1280,60,64,1]{0,2,1,3:T(8,128)} %fusion.148, f32[1280,60,64,1]{0,2,1,3:T(8,128)} %fusion.150, bf16[12,64,20,64]{1,3,2,0:T(8,128)(2,1)} %convert_bitcast_fusion, bf16[12,64,20,64]{1,3,2,0:T(8,128)(2,1)} %convert_bitcast_fusion.1, ...), kind=kOutput, calls=%fused_computation.35 | convolution fusion | flops 7588085760 | bytes 92411392 | tf_op jit(solution)/shard_map/bsd,bshe->dhe/dot_general | solution.py:69
  1059.9 12.8 bitcast_convert_fusion
  1072.8 13.8 fusion.161
  1091.6 648.5 %all-reduce.3.cloned.1.call-done = (f32[1280,60,64]{0,2,1:T(8,128)}, f32[20,64,1280]{2,1,0:T(8,128)}, f32[1280,5120]{1,0:T(8,128)}, f32[5120,1280]{1,0:T(8,128)}) async-done(((f32[1280,60,64]{0,2,1:T(8,128)}, f32[20,64,1280]{2,1,0:T(8,128)}, f32[1280,5120]{1,0:T(8,128)}, f32[5120,1280]{1,0:T(8,128)}), (f32[1280,60,64]{0,2,1:T(8,128)}, f32[20,64,1280]{2,1,0:T(8,128)}, f32[1280,5120]{1,0:T(8,128)}, ...) | async-done | bytes 78643216 | tf_op jit(solution)/shard_map/psum | solution.py:103
  1740.1 14.4 fusion.406
  1757.9 21.1 %copy.133 = f32[1280,5120]{1,0:T(8,128)} copy(f32[1280,5120]{1,0:T(8,128)} %get-tuple-element.71) | data formatting | bytes 52428800
  1782.2 9.3 copy.134
  (314 shorter events, 266.5 us)
Async XLA Ops:
  7.2 81.6 %copy-start = (bf16[20,64,1280]{2,1,0:T(8,128)(2,1)S(1)}, bf16[20,64,1280]{2,1,0:T(8,128)(2,1)}, u32[]{:S(2)}) copy-start(bf16[20,64,1280]{2,1,0:T(8,128)(2,1)} %param.15) | copy-start | bytes 9830404
  7.2 1732.9 %all-reduce.3.cloned.1.call-start = ((), (), s32[]{:S(2)}) async-start(), calls=%async_computation | async-start | bytes 157286400 | tf_op jit(solution)/shard_map/psum | solution.py:103
  24.9 17.5 copy-start.86
  42.5 46.2 %copy-start.56 = (bf16[1280]{0:T(1024)(128)(2,1)}, bf16[1280]{0:T(1024)(128)(2,1)S(1)}, u32[]{:S(2)}) copy-start(bf16[1280]{0:T(1024)(128)(2,1)S(1)} %get-tuple-element.12) | copy-start | bytes 7684
  42.5 70.1 %copy-start.89 = (bf16[1280]{0:T(1024)(128)(2,1)}, bf16[1280]{0:T(1024)(128)(2,1)S(1)}, u32[]{:S(2)}) copy-start(bf16[1280]{0:T(1024)(128)(2,1)S(1)} %get-tuple-element.11) | copy-start | bytes 7684
  46.4 19.2 %copy-start.63 = (f32[12,64]{1,0:T(8,128)}, f32[12,64]{1,0:T(8,128)S(1)}, u32[]{:S(2)}) copy-start(f32[12,64]{1,0:T(8,128)S(1)} %fusion.369) | copy-start | bytes 9220
  96.5 16.1 copy-start.38
  96.5 16.1 copy-start.18
  112.6 21.4 %copy-start.7 = (bf16[12,64,5120]{2,1,0:T(8,128)(2,1)}, bf16[12,64,5120]{2,1,0:T(8,128)(2,1)S(1)}, u32[]{:S(2)}) copy-start(bf16[12,64,5120]{2,1,0:T(8,128)(2,1)S(1)} %fusion.85) | copy-start | bytes 23592964
  112.7 22.7 %copy-start.91 = (bf16[1280,20,64]{0,2,1:T(8,128)(2,1)S(1)}, bf16[1280,20,64]{0,2,1:T(8,128)(2,1)}, u32[]{:S(2)}) copy-start(bf16[1280,20,64]{0,2,1:T(8,128)(2,1)} %param.14) | copy-start | bytes 9830404
  202.6 30.6 %copy-start.57 = (bf16[1280]{0:T(1024)(128)(2,1)S(1)}, bf16[1280]{0:T(1024)(128)(2,1)}, u32[]{:S(2)}) copy-start(bf16[1280]{0:T(1024)(128)(2,1)} %copy-done.56) | copy-start | bytes 7684
  202.6 30.6 %copy-start.60 = (f32[12,64]{1,0:T(8,128)S(1)}, f32[12,64]{1,0:T(8,128)}, u32[]{:S(2)}) copy-start(f32[12,64]{1,0:T(8,128)} %fusion.365) | copy-start | bytes 9220
  296.0 21.4 %copy-start.103 = (bf16[12,64,5120]{2,1,0:T(8,128)(2,1)}, bf16[12,64,5120]{2,1,0:T(8,128)(2,1)S(1)}, u32[]{:S(2)}) copy-start(bf16[12,64,5120]{2,1,0:T(8,128)(2,1)S(1)} %fusion.79) | copy-start | bytes 23592964
  296.0 22.7 %copy-start.92 = (bf16[1280,20,64]{0,2,1:T(8,128)(2,1)S(1)}, bf16[1280,20,64]{0,2,1:T(8,128)(2,1)}, u32[]{:S(2)}) copy-start(bf16[1280,20,64]{0,2,1:T(8,128)(2,1)} %param.14) | copy-start | bytes 9830404
  367.6 48.6 %copy-start.68 = (f32[12,64]{1,0:T(8,128)}, f32[12,64]{1,0:T(8,128)S(1)}, u32[]{:S(2)}) copy-start(f32[12,64]{1,0:T(8,128)S(1)} %fusion.368) | copy-start | bytes 9220
  386.3 30.0 %copy-start.59 = (f32[12,64]{1,0:T(8,128)S(1)}, f32[12,64]{1,0:T(8,128)}, u32[]{:S(2)}) copy-start(f32[12,64]{1,0:T(8,128)} %multiply_multiply_fusion.4) | copy-start | bytes 9220
  386.3 30.0 %copy-start.66 = (f32[12,64]{1,0:T(8,128)S(1)}, f32[12,64]{1,0:T(8,128)}, u32[]{:S(2)}) copy-start(f32[12,64]{1,0:T(8,128)} %copy-done.65) | copy-start | bytes 9220
  416.3 18.4 %slice-start.6 = ((s8[7864320]{0:T(1024)(128)(4,1)}), s8[4194304]{0:T(1024)(128)(4,1)S(1)}, s32[]{:S(2)}) async-start(s8[7864320]{0:T(1024)(128)(4,1)} %bitcast.399), calls=%async_computation.7 | async-start | bytes 8388608
  458.2 28.0 %slice-start.4 = ((s8[7864320]{0:T(1024)(128)(4,1)}), s8[4194304]{0:T(1024)(128)(4,1)S(1)}, s32[]{:S(2)}) async-start(s8[7864320]{0:T(1024)(128)(4,1)} %bitcast.397), calls=%async_computation.5 | async-start | bytes 8388608
  464.6 21.6 %slice-start.5 = ((s8[7864320]{0:T(1024)(128)(4,1)}), s8[3670016]{0:T(1024)(128)(4,1)S(1)}, s32[]{:S(2)}) async-start(s8[7864320]{0:T(1024)(128)(4,1)} %bitcast.397), calls=%async_computation.6 | async-start | bytes 7340032
  548.8 14.4 copy-start.84
  548.8 14.4 copy-start.101
  563.2 14.7 copy-start.75
  563.2 14.7 copy-start.88
  563.2 14.7 copy-start.16
  563.2 14.7 copy-start.28
  563.2 14.7 copy-start.33
  563.3 14.7 copy-start.82
  598.0 30.4 %copy-start.71 = (f32[12,64]{1,0:T(8,128)S(1)}, f32[12,64]{1,0:T(8,128)}, u32[]{:S(2)}) copy-start(f32[12,64]{1,0:T(8,128)} %copy-done.70) | copy-start | bytes 9220
  598.0 30.4 %copy-start.39 = (f32[12,64]{1,0:T(8,128)S(1)}, f32[12,64]{1,0:T(8,128)}, u32[]{:S(2)}) copy-start(f32[12,64]{1,0:T(8,128)} %copy-done.38) | copy-start | bytes 9220
  694.2 30.0 %copy-start.73 = (f32[12,64]{1,0:T(8,128)S(1)}, f32[12,64]{1,0:T(8,128)}, u32[]{:S(2)}) copy-start(f32[12,64]{1,0:T(8,128)} %copy-done.72) | copy-start | bytes 9220
  694.2 30.0 %copy-start.79 = (f32[12,64]{1,0:T(8,128)S(1)}, f32[12,64]{1,0:T(8,128)}, u32[]{:S(2)}) copy-start(f32[12,64]{1,0:T(8,128)} %copy-done.78) | copy-start | bytes 9220
  724.1 16.1 slice-start.2
  773.6 27.2 %copy-start.23 = (bf16[12,64,1280]{2,1,0:T(8,128)(2,1)S(1)}, bf16[12,64,1280]{2,1,0:T(8,128)(2,1)}, u32[]{:S(2)}) copy-start(bf16[12,64,1280]{2,1,0:T(8,128)(2,1)} %copy-done.22) | copy-start | bytes 5898244
  773.6 27.2 %copy-start.67 = (f32[12,64]{1,0:T(8,128)S(1)}, f32[12,64]{1,0:T(8,128)}, u32[]{:S(2)}) copy-start(f32[12,64]{1,0:T(8,128)} %copy-done.65) | copy-start | bytes 9220
  800.8 26.7 %copy-start.69 = (f32[12,64]{1,0:T(8,128)S(1)}, f32[12,64]{1,0:T(8,128)}, u32[]{:S(2)}) copy-start(f32[12,64]{1,0:T(8,128)} %copy-done.68) | copy-start | bytes 9220
  827.5 27.0 %copy-start.17 = (bf16[12,64,1280]{2,1,0:T(8,128)(2,1)S(1)}, bf16[12,64,1280]{2,1,0:T(8,128)(2,1)}, u32[]{:S(2)}) copy-start(bf16[12,64,1280]{2,1,0:T(8,128)(2,1)} %fusion.334) | copy-start | bytes 5898244
  854.4 20.8 %copy-start.20 = (bf16[24,64,1280]{2,1,0:T(8,128)(2,1)S(1)}, bf16[24,64,1280]{2,1,0:T(8,128)(2,1)}, u32[]{:S(2)}) copy-start(bf16[24,64,1280]{2,1,0:T(8,128)(2,1)} %param.10) | copy-start | bytes 11796484
  895.3 20.3 %copy-start.9 = (bf16[12,64,1280]{2,1,0:T(8,128)(2,1)S(1)}, bf16[12,64,1280]{2,1,0:T(8,128)(2,1)}, u32[]{:S(2)}) copy-start(bf16[12,64,1280]{2,1,0:T(8,128)(2,1)} %copy-done.8) | copy-start | bytes 5898244
  895.3 20.3 %copy-start.97 = (bf16[12,20,64,64]{3,2,1,0:T(8,128)(2,1)S(1)}, bf16[12,20,64,64]{3,2,1,0:T(8,128)(2,1)}, u32[]{:S(2)}) copy-start(bf16[12,20,64,64]{3,2,1,0:T(8,128)(2,1)} %convolution_convert_fusion.5) | copy-start | bytes 5898244
  987.0 40.2 %copy-start.64 = (f32[12,64]{1,0:T(8,128)S(1)}, f32[12,64]{1,0:T(8,128)}, u32[]{:S(2)}) copy-start(f32[12,64]{1,0:T(8,128)} %copy-done.63) | copy-start | bytes 9220
  1754.5 24.5 %slice-start.8 = ((s8[26214400]{0:T(1024)(128)(4,1)}), s8[1048576]{0:T(1024)(128)(4,1)S(1)}, s32[]{:S(2)}) async-start(s8[26214400]{0:T(1024)(128)(4,1)} %bitcast.401), calls=%async_computation.9 | async-start | bytes 2097152
  1754.5 24.5 %slice-start.9 = ((s8[26214400]{0:T(1024)(128)(4,1)}), s8[4194304]{0:T(1024)(128)(4,1)S(1)}, s32[]{:S(2)}) async-start(s8[26214400]{0:T(1024)(128)(4,1)} %bitcast.401), calls=%async_computation.10 | async-start | bytes 8388608
  1757.8 21.2 %slice-start.10 = ((s8[26214400]{0:T(1024)(128)(4,1)}), s8[4194304]{0:T(1024)(128)(4,1)S(1)}, s32[]{:S(2)}) async-start(s8[26214400]{0:T(1024)(128)(4,1)} %bitcast.401), calls=%async_computation.11 | async-start | bytes 8388608
  1757.8 21.2 %slice-start.11 = ((s8[26214400]{0:T(1024)(128)(4,1)}), s8[4194304]{0:T(1024)(128)(4,1)S(1)}, s32[]{:S(2)}) async-start(s8[26214400]{0:T(1024)(128)(4,1)} %bitcast.401), calls=%async_computation.12 | async-start | bytes 8388608
  1757.8 21.2 %slice-start.12 = ((s8[26214400]{0:T(1024)(128)(4,1)}), s8[4194304]{0:T(1024)(128)(4,1)S(1)}, s32[]{:S(2)}) async-start(s8[26214400]{0:T(1024)(128)(4,1)} %bitcast.401), calls=%async_computation.13 | async-start | bytes 8388608
  1757.8 23.1 %slice-start.13 = ((s8[26214400]{0:T(1024)(128)(4,1)}), s8[4194304]{0:T(1024)(128)(4,1)S(1)}, s32[]{:S(2)}) async-start(s8[26214400]{0:T(1024)(128)(4,1)} %bitcast.401), calls=%async_computation.14 | async-start | bytes 8388608
  1757.8 24.3 %slice-start.14 = ((s8[26214400]{0:T(1024)(128)(4,1)}), s8[4194304]{0:T(1024)(128)(4,1)S(1)}, s32[]{:S(2)}) async-start(s8[26214400]{0:T(1024)(128)(4,1)} %bitcast.401), calls=%async_computation.15 | async-start | bytes 8388608
  (73 other events, 562.3 us)
Sparse Core Ops, SparseCore 0:
  1060.0 680.0 all-reduce.2
where the time goes:
time: 1810 us; the launch traced here: 1800 us
  matrix products  976 us (54%)
  waiting for transfers between devices  649 us (36%)
  local copies, waits for them, and re-layouts  79.8 us (4%)
  other arithmetic  78.7 us (4%)
    psum x1, waiting for transfers between devices, per_device(): reduced = lax.psum(micro_grads, 'data')  649 us
    dot_general x4, matrix products, layer_bwd(): jnp.einsum('bsd,bsf->df', m_norm, d_up, preferred_element_type=jnp.float32)  126 us
    dot_general x4, matrix products, layer_bwd(): jnp.einsum('bsf,df->bsd', d_up, w_up, preferred_element_type=jnp.float32)  120 us
    dot_general x4, matrix products, layer_bwd(): jnp.einsum('bsf,bsd->fd', g_act, d_out, preferred_element_type=jnp.float32)  101 us
    dot_general x4, matrix products, layer_fwd(): jnp.einsum('bsd,dhe->bshe', u_norm, w_qkv, preferred_element_type=jnp.flo...  77.7 us
    dot_general x4, matrix products, layer_bwd(): jnp.einsum('bsd,bshe->dhe', u_norm, d_qkv, preferred_element_type=jnp.flo...  75 us
    dot_general x4, matrix products, layer_bwd(): jnp.einsum('bsd,fd->bsf', d_out, w_down, preferred_element_type=jnp.float32)  70.4 us
    unnamed x243, local copies, waits for them, and re-layouts  65.3 us
  transfers between devices with their start and end apart: 1, of which 1 were waited for; matrix products, arithmetic and copies ran while one was open for 2% of the time, Pallas kernels for 0%

commit v1 on v0

v1 whole, which is shorter than its diff:
```python
import jax
import jax.numpy as jnp
from jax import lax
from jax.sharding import PartitionSpec as P
import functools

NORM_EPS = 1e-6


def rms_norm(x_val):
    x_f32 = x_val.astype(jnp.float32)
    return (x_f32 * lax.rsqrt(jnp.mean(x_f32 * x_f32, axis=-1, keepdims=True) + NORM_EPS)).astype(jnp.bfloat16)


def gelu_act(z_val):
    return jax.nn.gelu(z_val.astype(jnp.float32), approximate=True).astype(jnp.bfloat16)


def attn_probs(scores, attn_scale):
    return jax.nn.softmax(scores.astype(jnp.float32) * attn_scale, axis=-1).astype(jnp.bfloat16)


def mm(spec, a, b):
    return jnp.einsum(spec, a, b, preferred_element_type=jnp.float32).astype(jnp.bfloat16)


def layer_fwd(x_prev, step_vec, weights, scale):
    w_q, w_k, w_v, w_o, w_up, w_down = weights
    x_cur = x_prev + step_vec
    u = rms_norm(x_cur)
    q, k, v = (mm('bsd,dhe->bhse', u, w) for w in (w_q, w_k, w_v))
    scores = mm('bhqe,bhke->bhqk', q, k)
    prob = attn_probs(scores, scale)
    mix = mm('bhqk,bhke->bhqe', prob, v)
    h = x_cur + mm('bhqe,hed->bqd', mix, w_o)
    z = mm('bsd,df->bsf', rms_norm(h), w_up)
    y = mm('bsf,fd->bsd', gelu_act(z), w_down)
    return h + y, (x_cur, q, k, v, scores, mix, h, z)


def solution(mesh):
    batch_spec = P('data', None, None)

    def per_device(x_loc, g_loc, step_emb, w_q, w_k, w_v, w_o, w_up, w_down):
        scale = w_q.shape[2] ** -0.5
        weights = (w_q, w_k, w_v, w_o, w_up, w_down)
        n_layers = step_emb.shape[0]
        x, saved = x_loc, []
        for l in range(n_layers):
            x, s = layer_fwd(x, step_emb[l], weights, scale)
            saved.append(s)
        d_out = g_loc
        acts = {k: [] for k in ('down', 'up', 'o', 'q', 'k', 'v')}
        for l in reversed(range(n_layers)):
            x_cur, q, k, v, scores, mix, h, z = saved[l]
            g_act, gelu_pull = jax.vjp(gelu_act, z)
            acts['down'].append((g_act, d_out))
            (d_up,) = gelu_pull(mm('bsd,fd->bsf', d_out, w_down))
            m, pull_h = jax.vjp(rms_norm, h)
            acts['up'].append((m, d_up))
            (d_h,) = pull_h(mm('bsf,df->bsd', d_up, w_up))
            d_mid = d_out + d_h
            acts['o'].append((mix, d_mid))
            d_mix = mm('bqd,hed->bhqe', d_mid, w_o)
            prob, prob_pull = jax.vjp(functools.partial(attn_probs, attn_scale=scale), scores)
            d_v = mm('bhqk,bhqe->bhke', prob, d_mix)
            (d_s,) = prob_pull(mm('bhqe,bhke->bhqk', d_mix, v))
            d_q = mm('bhqk,bhke->bhqe', d_s, k)
            d_k = mm('bhqk,bhqe->bhke', d_s, q)
            u, pull_x = jax.vjp(rms_norm, x_cur)
            for n, d in (('q', d_q), ('k', d_k), ('v', d_v)):
                acts[n].append((u, d))
            d_u = (jnp.einsum('bhse,dhe->bsd', d_q, w_q, preferred_element_type=jnp.float32)
                   + jnp.einsum('bhse,dhe->bsd', d_k, w_k, preferred_element_type=jnp.float32)
                   + jnp.einsum('bhse,dhe->bsd', d_v, w_v, preferred_element_type=jnp.float32))
            (d_x,) = pull_x(d_u.astype(jnp.bfloat16))
            d_out = d_mid + d_x

        def wgrad(spec, pairs):
            return sum(jnp.einsum(spec, a, b, preferred_element_type=jnp.float32) for a, b in pairs)

        def reduce(g):
            flat = g.reshape(-1, g.shape[-1])
            part = lax.psum_scatter(flat, 'data', scatter_dimension=0, tiled=True)
            return lax.all_gather(part, 'data', axis=0, tiled=True).reshape(g.shape)

        grad_down = reduce(wgrad('bsf,bsd->fd', acts['down']))
        grad_up = reduce(wgrad('bsd,bsf->df', acts['up']))
        grad_o = reduce(wgrad('bhse,bsd->hed', acts['o']))
        gq, gk, gv = (reduce(wgrad('bsd,bhse->hed', acts[n])).transpose(2, 0, 1) for n in 'qkv')
        return gq, gk, gv, grad_o, grad_up, grad_down, d_out

    return jax.shard_map(per_device, mesh=mesh, in_specs=(batch_spec, batch_spec, P(), P(), P(), P(), P(), P(), P()), out_specs=(P(), P(), P(), P(), P(), P(), batch_spec), check_vma=False)
```

time: 1810 us -> 1940 us (1.072)
  waiting for transfers between devices: 649 us -> 981 us
  matrix products: 976 us -> 798 us
    psum x1 -> x0, waiting for transfers between devices: 649 us -> none  [per_device(): reduced = lax.psum(micro_grads, 'data')]
    reduce_scatter x0 -> x6, waiting for transfers between devices: none -> 620 us  [reduce(): part = lax.psum_scatter(flat, 'data', scatter_dimension=0, tiled=True)]
    all_gather x0 -> x6, waiting for transfers between devices: none -> 358 us  [reduce(): return lax.all_gather(part, 'data', axis=0, tiled=True).reshape(g.shape)]
    dot_general x70 -> x47, matrix products: 976 us -> 798 us  [the longest x29 502 us: mm(): jnp.einsum(spec, a, b, preferred_element_type=jnp.float32)]
    unnamed x243 -> x146, local copies, waits for them, and re-layouts: 65.3 us -> 65.8 us
  transfers between devices with their start and end apart: 1 -> 12, of which waited for: 1 -> 9; matrix products, arithmetic and copies ran while one was open for 2% -> 14% of each run, Pallas kernels for 0% -> 0%
where the time goes in v1:
time: 1940 us
  waiting for transfers between devices  981 us (51%)
  matrix products  798 us (41%)
  other arithmetic  74.8 us (4%)
  local copies, waits for them, and re-layouts  67.3 us (3%)
    reduce_scatter x6, waiting for transfers between devices, reduce(): part = lax.psum_scatter(flat, 'data', scatter_dimension=0, tiled=True)  620 us
    dot_general x29, matrix products, mm(): jnp.einsum(spec, a, b, preferred_element_type=jnp.float32)  502 us
    all_gather x6, waiting for transfers between devices, reduce(): return lax.all_gather(part, 'data', axis=0, tiled=True).reshape(g.shape)  358 us
    dot_general x12, matrix products, wgrad(): jnp.einsum(spec, a, b, preferred_element_type=jnp.float32)  231 us
    unnamed x146, local copies, waits for them, and re-layouts  65.8 us
  transfers between devices with their start and end apart: 12, of which 9 were waited for; matrix products, arithmetic and copies ran while one was open for 14% of the time, Pallas kernels for 0%

profile of v1, /device:TPU:0, one launch (start us, length us, event | category | flops | bytes accessed | tf_op | source)
XLA Modules:
  0.0 1936.3 jit_solution(3684555897567985550)
XLA Ops:
  12.6 14.9 convolution_convert_fusion.5
  27.5 12.5 convolution_convert_fusion.6
  39.9 11.0 convolution_convert_fusion.7
  50.9 13.5 fusion.115
  64.4 14.7 fusion.232
  79.1 12.6 fusion.123
  91.7 10.9 fusion.71
  102.6 29.4 %fusion.58 = bf16[24,64,5120]{2,1,0:T(8,128)(2,1)} fusion(bf16[1280,5120]{1,0:T(8,128)(2,1)} %param.16, bf16[24,64,1280]{2,1,0:T(8,128)(2,1)S(1)} %get-tuple-element.12, f32[24,64]{1,0:T(8,128)S(1)} %fusion.206), kind=kOutput, calls=%fused_computation.97 | convolution fusion | flops 20146421760 | bytes 32774144 | tf_op jit(solution)/shard_map/bsd,df->bsf/dot_general | solution.py:24
  132.1 34.2 %fusion.74 = (f32[24,64]{1,0:T(8,128)S(1)}, bf16[24,64,1280]{2,1,0:T(8,128)(2,1)S(1)}) fusion(bf16[1280]{0:T(1024)(128)(2,1)S(1)} %copy-done.51, bf16[24,64,1280]{2,1,0:T(8,128)(2,1)S(1)} %get-tuple-element.12, bf16[5120,1280]{1,0:T(8,128)(2,1)} %param.17, bf16[24,64,5120]{2,1,0:T(8,128)(2,1)} %fusion.58), kind=kOutput, calls=%fused_computation.113 | convolution fusion | flops 20223096832 | bytes 36708864 | tf_op jit(solution)/shard_map/bsf,fd->bsd/dot_general | solution.py:24
  166.3 12.6 convolution_convert_fusion.3
  179.0 10.9 convolution_convert_fusion.4
  190.0 12.4 convolution_convert_fusion.2
  213.7 14.4 fusion.233
  228.9 12.5 fusion.137
  241.4 10.8 fusion.77
  252.3 29.4 %fusion.61 = bf16[24,64,5120]{2,1,0:T(8,128)(2,1)} fusion(bf16[1280,5120]{1,0:T(8,128)(2,1)} %param.16, bf16[24,64,1280]{2,1,0:T(8,128)(2,1)S(1)} %get-tuple-element.18, f32[24,64]{1,0:T(8,128)S(1)} %fusion.208), kind=kOutput, calls=%fused_computation.98 | convolution fusion | flops 20146421760 | bytes 32774144 | tf_op jit(solution)/shard_map/bsd,df->bsf/dot_general | solution.py:24
  281.8 43.6 %fusion.6 = bf16[24,64,5120]{2,1,0:T(8,128)(2,1)} fusion(bf16[24,64,5120]{2,1,0:T(8,128)(2,1)} %fusion.61, bf16[24,64,1280]{2,1,0:T(8,128)(2,1)S(1)} %copy-done.25, bf16[5120,1280]{1,0:T(8,128)(2,1)} %param.17), kind=kOutput, calls=%fused_computation.18 | convolution fusion | flops 20313538560 | bytes 48496640 | tf_op jit(solution)/shard_map/bsd,fd->bsf/dot_general | solution.py:24
  325.4 28.7 %fusion.79 = (f32[24,64]{1,0:T(8,128)S(1)}, bf16[24,64,1280]{2,1,0:T(8,128)(2,1)}) fusion(bf16[24,64,1280]{2,1,0:T(8,128)(2,1)} %copy-done.26, bf16[24,64,5120]{2,1,0:T(8,128)(2,1)} %fusion.6, bf16[1280,5120]{1,0:T(8,128)(2,1)} %param.16), kind=kOutput, calls=%fused_computation.118 | convolution fusion | flops 20142487552 | bytes 36706304 | tf_op jit(solution)/shard_map/bsf,df->bsd/dot_general | solution.py:24
  384.2 16.3 fusion.28
  423.7 11.0 fusion.126
  434.8 11.4 fusion.221
  462.3 14.2 fusion.76
  482.4 43.5 %fusion.9 = bf16[24,64,5120]{2,1,0:T(8,128)(2,1)} fusion(bf16[24,64,5120]{2,1,0:T(8,128)(2,1)} %fusion.58, bf16[24,64,1280]{2,1,0:T(8,128)(2,1)S(1)} %fusion.169, bf16[5120,1280]{1,0:T(8,128)(2,1)} %param.17), kind=kOutput, calls=%fused_computation.21 | convolution fusion | flops 20313538560 | bytes 48496640 | tf_op jit(solution)/shard_map/bsd,fd->bsf/dot_general | solution.py:24
  525.9 28.7 %fusion.73 = (f32[24,64]{1,0:T(8,128)S(1)}, bf16[24,64,1280]{2,1,0:T(8,128)(2,1)}) fusion(bf16[24,64,1280]{2,1,0:T(8,128)(2,1)} %copy-done.12, bf16[24,64,5120]{2,1,0:T(8,128)(2,1)} %fusion.9, bf16[1280,5120]{1,0:T(8,128)(2,1)} %param.16), kind=kOutput, calls=%fused_computation.112 | convolution fusion | flops 20142487552 | bytes 36706304 | tf_op jit(solution)/shard_map/bsf,df->bsd/dot_general | solution.py:24
  562.2 12.2 convolution_convert_fusion
  574.4 16.3 fusion.33
  601.7 12.0 fusion.120
  613.7 12.8 bitcast_add_fusion.9
  626.6 11.7 fusion.219
  649.1 12.3 bitcast_add_fusion.8
  661.4 11.4 fusion.217
  672.9 12.4 fusion.153
  685.3 12.9 bitcast_add_fusion.7
  718.4 28.6 %fusion.180 = f32[1280,5120,1]{1,0,2:T(8,128)} fusion(bf16[24,64,5120]{2,1,0:T(8,128)(2,1)} %fusion.6, bf16[24,64,1280]{2,1,0:T(8,128)(2,1)} %copy-done.26, f32[24,64]{1,0:T(8,128)S(1)} %copy-done.44), kind=kOutput, calls=%fused_computation.198 | convolution fusion | flops 20138557440 | bytes 45881344 | tf_op jit(solution)/shard_map/bsd,bsf->df/dot_general | solution.py:80
  747.1 31.6 %bitcast_add_fusion.1 = f32[1280,5120]{1,0:T(8,128)} fusion(f32[1280,5120,1]{1,0,2:T(8,128)} %fusion.180, bf16[24,64,5120]{2,1,0:T(8,128)(2,1)} %fusion.9, bf16[24,64,1280]{2,1,0:T(8,128)(2,1)S(1)} %copy-done.13, f32[24,64]{1,0:T(8,128)S(1)} %copy-done.24), kind=kOutput, calls=%fused_computation.37 | convolution fusion | flops 20145111040 | bytes 72095744 | tf_op jit(solution)/shard_map/bsd,bsf->df/dot_general | solution.py:80
  778.8 43.3 %fusion.38 = f32[5120,1280,1]{1,0,2:T(8,128)} fusion(bf16[24,64,1280]{2,1,0:T(8,128)(2,1)} %param.10, bf16[24,64,5120]{2,1,0:T(8,128)(2,1)} %fusion.61), kind=kOutput, calls=%fused_computation.62 | convolution fusion | flops 20211302400 | bytes 45875200 | tf_op jit(solution)/shard_map/bsf,bsd->fd/dot_general | solution.py:80
  822.2 34.4 %bitcast_add_fusion = f32[5120,1280]{1,0:T(8,128)} fusion(f32[5120,1280,1]{1,0,2:T(8,128)} %fusion.38, bf16[24,64,1280]{2,1,0:T(8,128)(2,1)S(1)} %copy-done.21, bf16[24,64,5120]{2,1,0:T(8,128)(2,1)} %fusion.58), kind=kOutput, calls=%fused_computation.36 | convolution fusion | flops 20217856000 | bytes 72089600 | tf_op jit(solution)/shard_map/bsf,bsd->fd/dot_general | solution.py:80
  858.9 72.8 %reduce-scatter.13.cloned.1.call-done = f32[80,1280]{1,0:T(8,128)} async-done(((f32[1280,1280]{1,0:T(8,128)}), f32[80,1280]{1,0:T(8,128)}) %reduce-scatter.13.cloned.1.call-update) | async-done | bytes 409616 | tf_op jit(solution)/shard_map/reduce_scatter | solution.py:84
  931.8 273.9 %reduce-scatter.15.cloned.1.call-done = f32[80,5120]{1,0:T(8,128)} async-done(((f32[1280,5120]{1,0:T(8,128)}), f32[80,5120]{1,0:T(8,128)}) %reduce-scatter.15.cloned.1.call-update) | async-done | bytes 1638416 | tf_op jit(solution)/shard_map/reduce_scatter | solution.py:84
  1205.8 273.3 %reduce-scatter.17.cloned.1.call-done = f32[320,1280]{1,0:T(8,128)} async-done(((f32[5120,1280]{1,0:T(8,128)}), f32[320,1280]{1,0:T(8,128)}) %reduce-scatter.17.cloned.1.call-update) | async-done | bytes 1638416 | tf_op jit(solution)/shard_map/reduce_scatter | solution.py:84
  1479.1 11.2 fusion.193
  1500.5 13.2 fusion.70
  1522.2 45.0 %all-gather.9.cloned.1.call-done = f32[1280,1280]{1,0:T(8,128)} async-done(((f32[80,1280]{1,0:T(8,128)}), f32[1280,1280]{1,0:T(8,128)}) %all-gather.9.cloned.1.call-update) | async-done | bytes 6553616 | tf_op jit(solution)/shard_map/all_gather | solution.py:85
  1567.2 45.0 %all-gather.11.cloned.1.call-done = f32[1280,1280]{1,0:T(8,128)} async-done(((f32[80,1280]{1,0:T(8,128)}), f32[1280,1280]{1,0:T(8,128)}) %all-gather.11.cloned.1.call-update) | async-done | bytes 6553616 | tf_op jit(solution)/shard_map/all_gather | solution.py:85
  1612.2 44.8 %all-gather.13.cloned.1.call-done = f32[1280,1280]{1,0:T(8,128)} async-done(((f32[80,1280]{1,0:T(8,128)}), f32[1280,1280]{1,0:T(8,128)}) %all-gather.13.cloned.1.call-update) | async-done | bytes 6553616 | tf_op jit(solution)/shard_map/all_gather | solution.py:85
  1657.0 109.6 %all-gather.15.cloned.1.call-done = f32[1280,5120]{1,0:T(8,128)} async-done(((f32[80,5120]{1,0:T(8,128)}), f32[1280,5120]{1,0:T(8,128)}) %all-gather.15.cloned.1.call-update) | async-done | bytes 26214416 | tf_op jit(solution)/shard_map/all_gather | solution.py:85
  1766.6 109.4 %all-gather.17.cloned.1.call-done = f32[5120,1280]{1,0:T(8,128)} async-done(((f32[320,1280]{1,0:T(8,128)}), f32[5120,1280]{1,0:T(8,128)}) %all-gather.17.cloned.1.call-update) | async-done | bytes 26214416 | tf_op jit(solution)/shard_map/all_gather | solution.py:85
  1911.5 17.6 copy.63
  (205 shorter events, 198.8 us)
Async XLA Ops:
  7.2 84.6 %copy-start = (bf16[20,64,1280]{2,1,0:T(8,128)(2,1)S(1)}, bf16[20,64,1280]{2,1,0:T(8,128)(2,1)}, u32[]{:S(2)}) copy-start(bf16[20,64,1280]{2,1,0:T(8,128)(2,1)} %param.15) | copy-start | bytes 9830404
  7.2 849.5 %reduce-scatter.7.cloned.1.call-start = ((), (), s32[]{:S(2)}) async-start(), calls=%async_computation.6 | async-start | bytes 6963200 | tf_op jit(solution)/shard_map/reduce_scatter | solution.py:84
  8.7 83.0 %copy-start.38 = (bf16[1280]{0:T(1024)(128)(2,1)}, bf16[1280]{0:T(1024)(128)(2,1)S(1)}, u32[]{:S(2)}) copy-start(bf16[1280]{0:T(1024)(128)(2,1)S(1)} %get-tuple-element.8) | copy-start | bytes 7684
  12.5 27.4 %copy-start.32 = (f32[24,64]{1,0:T(8,128)}, f32[24,64]{1,0:T(8,128)S(1)}, u32[]{:S(2)}) copy-start(f32[24,64]{1,0:T(8,128)S(1)} %fusion.205) | copy-start | bytes 18436
  12.5 14.9 copy-start.3
  12.5 14.9 copy-start.52
  50.9 13.5 copy-start.7
  102.6 29.4 %copy-start.45 = (f32[24,64]{1,0:T(8,128)}, f32[24,64]{1,0:T(8,128)S(1)}, u32[]{:S(2)}) copy-start(f32[24,64]{1,0:T(8,128)S(1)} %get-tuple-element.11) | copy-start | bytes 18436
  102.6 29.4 %copy-start.12 = (bf16[24,64,1280]{2,1,0:T(8,128)(2,1)}, bf16[24,64,1280]{2,1,0:T(8,128)(2,1)S(1)}, u32[]{:S(2)}) copy-start(bf16[24,64,1280]{2,1,0:T(8,128)(2,1)S(1)} %get-tuple-element.12) | copy-start | bytes 11796484
  102.6 29.4 %copy-start.22 = (f32[24,64]{1,0:T(8,128)}, f32[24,64]{1,0:T(8,128)S(1)}, u32[]{:S(2)}) copy-start(f32[24,64]{1,0:T(8,128)S(1)} %fusion.206) | copy-start | bytes 18436
  102.6 29.4 %copy-start.51 = (bf16[1280]{0:T(1024)(128)(2,1)S(1)}, bf16[1280]{0:T(1024)(128)(2,1)}, u32[]{:S(2)}) copy-start(bf16[1280]{0:T(1024)(128)(2,1)} %get-tuple-element.7) | copy-start | bytes 7684
  132.1 34.2 %copy-start.53 = (bf16[1280,20,64]{0,2,1:T(8,128)(2,1)S(1)}, bf16[1280,20,64]{0,2,1:T(8,128)(2,1)}, u32[]{:S(2)}) copy-start(bf16[1280,20,64]{0,2,1:T(8,128)(2,1)} %param.13) | copy-start | bytes 9830404
  166.3 23.6 %copy-start.9 = (bf16[24,64,1280]{2,1,0:T(8,128)(2,1)}, bf16[24,64,1280]{2,1,0:T(8,128)(2,1)S(1)}, u32[]{:S(2)}) copy-start(bf16[24,64,1280]{2,1,0:T(8,128)(2,1)S(1)} %get-tuple-element.14) | copy-start | bytes 11796484
  166.3 23.6 %copy-start.35 = (f32[24,64]{1,0:T(8,128)}, f32[24,64]{1,0:T(8,128)S(1)}, u32[]{:S(2)}) copy-start(f32[24,64]{1,0:T(8,128)S(1)} %fusion.207) | copy-start | bytes 18436
  189.9 13.2 copy-start.8
  228.1 13.3 copy-start.30
  252.3 29.5 %copy-start.26 = (bf16[24,64,1280]{2,1,0:T(8,128)(2,1)}, bf16[24,64,1280]{2,1,0:T(8,128)(2,1)S(1)}, u32[]{:S(2)}) copy-start(bf16[24,64,1280]{2,1,0:T(8,128)(2,1)S(1)} %get-tuple-element.18) | copy-start | bytes 11796484
  252.3 29.5 %copy-start.49 = (f32[24,64]{1,0:T(8,128)}, f32[24,64]{1,0:T(8,128)S(1)}, u32[]{:S(2)}) copy-start(f32[24,64]{1,0:T(8,128)S(1)} %get-tuple-element.17) | copy-start | bytes 18436
  252.3 101.8 %copy-start.43 = (f32[24,64]{1,0:T(8,128)}, f32[24,64]{1,0:T(8,128)S(1)}, u32[]{:S(2)}) copy-start(f32[24,64]{1,0:T(8,128)S(1)} %fusion.208) | copy-start | bytes 18436
  252.3 29.4 %copy-start.25 = (bf16[24,64,1280]{2,1,0:T(8,128)(2,1)S(1)}, bf16[24,64,1280]{2,1,0:T(8,128)(2,1)}, u32[]{:S(2)}) copy-start(bf16[24,64,1280]{2,1,0:T(8,128)(2,1)} %param.10) | copy-start | bytes 11796484
  325.4 28.7 %copy-start.50 = (f32[24,64]{1,0:T(8,128)S(1)}, f32[24,64]{1,0:T(8,128)}, u32[]{:S(2)}) copy-start(f32[24,64]{1,0:T(8,128)} %copy-done.49) | copy-start | bytes 18436
  361.6 13.9 copy-start.31
  434.7 19.3 slice-start
  462.3 14.2 copy-start.48
  462.3 14.3 copy-start.15
  525.9 28.7 %copy-start.46 = (f32[24,64]{1,0:T(8,128)S(1)}, f32[24,64]{1,0:T(8,128)}, u32[]{:S(2)}) copy-start(f32[24,64]{1,0:T(8,128)} %copy-done.45) | copy-start | bytes 18436
  525.9 28.8 %copy-start.23 = (f32[24,64]{1,0:T(8,128)S(1)}, f32[24,64]{1,0:T(8,128)}, u32[]{:S(2)}) copy-start(f32[24,64]{1,0:T(8,128)} %copy-done.22) | copy-start | bytes 18436
  626.5 230.9 %reduce-scatter.9.cloned.1.call-start = ((), (), s32[]{:S(2)}) async-start(), calls=%async_computation.8 | async-start | bytes 6963200 | tf_op jit(solution)/shard_map/reduce_scatter | solution.py:84
  661.4 196.8 %reduce-scatter.11.cloned.1.call-start = ((), (), s32[]{:S(2)}) async-start(), calls=%async_computation.10 | async-start | bytes 6963200 | tf_op jit(solution)/shard_map/reduce_scatter | solution.py:84
  698.2 233.5 %reduce-scatter.13.cloned.1.call-start = ((), (), s32[]{:S(2)}) async-start(), calls=%async_computation.12 | async-start | bytes 6963200 | tf_op jit(solution)/shard_map/reduce_scatter | solution.py:84
  718.3 28.7 %copy-start.24 = (f32[24,64]{1,0:T(8,128)S(1)}, f32[24,64]{1,0:T(8,128)}, u32[]{:S(2)}) copy-start(f32[24,64]{1,0:T(8,128)} %copy-done.22) | copy-start | bytes 18436
  718.4 487.3 %reduce-scatter.15.cloned.1.call-start = ((), (), s32[]{:S(2)}) async-start(), calls=%async_computation.14 | async-start | bytes 27852800 | tf_op jit(solution)/shard_map/reduce_scatter | solution.py:84
  718.4 28.7 %copy-start.13 = (bf16[24,64,1280]{2,1,0:T(8,128)(2,1)S(1)}, bf16[24,64,1280]{2,1,0:T(8,128)(2,1)}, u32[]{:S(2)}) copy-start(bf16[24,64,1280]{2,1,0:T(8,128)(2,1)} %copy-done.12) | copy-start | bytes 11796484
  778.7 700.3 %reduce-scatter.17.cloned.1.call-start = ((), (), s32[]{:S(2)}) async-start(), calls=%async_computation.16 | async-start | bytes 27852800 | tf_op jit(solution)/shard_map/reduce_scatter | solution.py:84
  778.8 43.4 %copy-start.21 = (bf16[24,64,1280]{2,1,0:T(8,128)(2,1)S(1)}, bf16[24,64,1280]{2,1,0:T(8,128)(2,1)}, u32[]{:S(2)}) copy-start(bf16[24,64,1280]{2,1,0:T(8,128)(2,1)} %copy-done.20) | copy-start | bytes 11796484
  856.6 665.6 %all-gather.7.cloned.1.call-start = ((), (), s32[]{:S(2)}) async-start(), calls=%async_computation.7 | async-start | bytes 6963200 | tf_op jit(solution)/shard_map/all_gather | solution.py:85
  857.4 709.9 %all-gather.9.cloned.1.call-start = ((), (), s32[]{:S(2)}) async-start(), calls=%async_computation.9 | async-start | bytes 6963200 | tf_op jit(solution)/shard_map/all_gather | solution.py:85
  858.1 754.1 %all-gather.11.cloned.1.call-start = ((), (), s32[]{:S(2)}) async-start(), calls=%async_computation.11 | async-start | bytes 6963200 | tf_op jit(solution)/shard_map/all_gather | solution.py:85
  858.8 798.2 %all-gather.13.cloned.1.call-start = ((), (), s32[]{:S(2)}) async-start(), calls=%async_computation.13 | async-start | bytes 6963200 | tf_op jit(solution)/shard_map/all_gather | solution.py:85
  931.7 834.9 %all-gather.15.cloned.1.call-start = ((), (), s32[]{:S(2)}) async-start(), calls=%async_computation.15 | async-start | bytes 27852800 | tf_op jit(solution)/shard_map/all_gather | solution.py:85
  1205.7 670.3 %all-gather.17.cloned.1.call-start = ((), (), s32[]{:S(2)}) async-start(), calls=%async_computation.17 | async-start | bytes 27852800 | tf_op jit(solution)/shard_map/all_gather | solution.py:85
  1500.5 13.2 copy-start.42
  1500.5 13.3 copy-start.18
  1500.5 13.3 copy-start.34
  1876.0 26.1 %slice-start.2 = ((s8[26214400]{0:T(1024)(128)(4,1)}), s8[4194304]{0:T(1024)(128)(4,1)S(1)}, s32[]{:S(2)}) async-start(s8[26214400]{0:T(1024)(128)(4,1)} %bitcast.304), calls=%async_computation.20 | async-start | bytes 8388608
  1876.0 26.1 %slice-start.3 = ((s8[26214400]{0:T(1024)(128)(4,1)}), s8[4194304]{0:T(1024)(128)(4,1)S(1)}, s32[]{:S(2)}) async-start(s8[26214400]{0:T(1024)(128)(4,1)} %bitcast.304), calls=%async_computation.21 | async-start | bytes 8388608
  1882.6 19.5 %slice-start.4 = ((s8[26214400]{0:T(1024)(128)(4,1)}), s8[4194304]{0:T(1024)(128)(4,1)S(1)}, s32[]{:S(2)}) async-start(s8[26214400]{0:T(1024)(128)(4,1)} %bitcast.304), calls=%async_computation.22 | async-start | bytes 8388608
  1882.6 19.5 %slice-start.5 = ((s8[26214400]{0:T(1024)(128)(4,1)}), s8[4194304]{0:T(1024)(128)(4,1)S(1)}, s32[]{:S(2)}) async-start(s8[26214400]{0:T(1024)(128)(4,1)} %bitcast.304), calls=%async_computation.23 | async-start | bytes 8388608
  (34 other events, 321.4 us)
Sparse Core Ops, SparseCore 0:
  626.7 77.0 reduce-scatter.6
  706.6 73.1 reduce-scatter.8
  782.7 73.1 reduce-scatter.10
  858.5 73.1 reduce-scatter.12
  934.4 271.2 reduce-scatter.14
  1208.4 270.6 reduce-scatter.16
  1481.3 40.9 all-gather.6
  1524.5 42.6 all-gather.8
  1569.5 42.6 all-gather.10
  1614.3 42.6 all-gather.12
  1659.2 107.2 all-gather.14
  1768.7 107.2 all-gather.16
